TPU v7x, 32 devices: a whole 2x2x4 slice. The times are simulated.
32 devices in a mesh: section: 4 (over x, core), tp: 8 (over z, y).
Axes of the slice: x: 2, y: 2, z: 4, core: 2. Of those that a mesh axis runs over, the one named last changes fastest.
Arguments:
- pending_activation: bfloat16 [4, 128, 4096], P('section'), may hold values from -6 to 6
- admissible_microbatches: bfloat16 [4, 128, 4096], P(None, None, 'tp'), may hold values from -6 to 6
- arrival_plan: int32 [4], replicated, may hold values from 0 to 3, each once
- vanished_hop: int32 [1], replicated, may hold values from 1 to 3
- query_key_value_matrices: bfloat16 [4, 4096, 3, 2048], P('section', None, None, 'tp')
- mixing_projection_matrices: bfloat16 [4, 2048, 4096], P('section', 'tp'), may hold values from -0.125 to 0.125
- normalizer_factors: bfloat16 [4, 4096], P('section'), may hold values from 0.25 to 1.75
Outputs:
- activation_later: bfloat16 [4, 128, 4096], P('section')
- standby_input: bfloat16 [4, 128, 4096], P('section', None, 'tp')
Inputs may be any that keep to these rules, and one draw needn't show every extreme that they name: `vanished_hop`: the preempted section is not the first. `arrival_plan`: each micro-batch index once.
All inputs are finite; a program needn't handle non-finite values.
Results may differ from a plain program's by a relative error of at most 0.013.
Values may be sent and summed in bfloat16 or wider, within the bound.
A program may use at most 64 MiB of HBM per device.

v0:
```python
import jax
import jax.numpy as jnp
from jax import lax
from jax.sharding import PartitionSpec as P

HD = 128
TICKS = 3
NORM_EPS = 1e-05


def shifted(value, axis, steps):
    count = lax.axis_size(axis)
    pairs = [(source, (source + steps) % count) for source in range(count)]
    return lax.ppermute(value, axis, pairs)


def layer_norm(x_rows, scale_row):
    widened = x_rows.astype(jnp.float32)
    row_mean = jnp.mean(widened, axis=-1, keepdims=True)
    centered = widened - row_mean
    row_var = jnp.mean(centered * centered, axis=-1, keepdims=True)
    return (centered * lax.rsqrt(row_var + NORM_EPS) * scale_row.astype(jnp.float32)).astype(
        jnp.bfloat16
    )


def attend(normed, w_in, w_out):
    row_count = normed.shape[0]
    col_count = w_in.shape[2]
    head_count = col_count // HD
    projected = jnp.dot(
        normed, w_in.reshape(w_in.shape[0], 3 * col_count), preferred_element_type=jnp.float32
    )
    projected = projected.astype(jnp.bfloat16).reshape(row_count, 3, head_count, HD)
    queries = projected[:, 0]
    key_rows = projected[:, 1]
    values = projected[:, 2]
    scores = jnp.einsum(
        "qhd,khd->hqk", queries, key_rows, preferred_element_type=jnp.float32
    ) * HD ** (-0.5)
    causal = jnp.arange(row_count)[:, None] >= jnp.arange(row_count)[None, :]
    scores = jnp.where(causal[None], scores, -jnp.inf)
    row_max = jnp.max(scores, axis=-1, keepdims=True)
    weights = jnp.exp(scores - row_max)
    probs = (weights / jnp.sum(weights, axis=-1, keepdims=True)).astype(jnp.bfloat16)
    context = jnp.einsum("hqk,khd->qhd", probs, values, preferred_element_type=jnp.float32)
    context = context.astype(jnp.bfloat16).reshape(row_count, col_count)
    return jnp.dot(context, w_out, preferred_element_type=jnp.float32)


def per_device(
    pending_activation,
    admissible_microbatches,
    arrival_plan,
    vanished_hop,
    query_key_value_matrices,
    mixing_projection_matrices,
    normalizer_factors,
):
    sections = lax.axis_size("section")
    my_section = lax.axis_index("section")
    sharding_degree = lax.axis_size("tp")
    slice_breadth = pending_activation.shape[2] // sharding_degree
    col_start = lax.axis_index("tp") * slice_breadth
    lost_at = vanished_hop[0]
    is_pred = my_section == lost_at - 1
    is_next = my_section == lost_at + 1
    is_lost = my_section == lost_at
    w_in = query_key_value_matrices[0]
    w_out = mixing_projection_matrices[0]
    scale_row = normalizer_factors[0]
    entire_source_lines = pending_activation[0]
    x_sh = lax.dynamic_slice_in_dim(entire_source_lines, col_start, slice_breadth, 1)
    blank = jnp.zeros(entire_source_lines.shape, jnp.float32)
    far_in, far_out, far_gain = shifted((w_in, w_out, scale_row), "section", -1)

    def successor_layer(rows_full):
        return attend(layer_norm(rows_full, far_gain), far_in, far_out)

    standby_sh = x_sh
    for tick_index in range(TICKS):
        own_part = attend(layer_norm(entire_source_lines, scale_row), w_in, w_out)
        ya_sh = (
            x_sh.astype(jnp.float32)
            + lax.psum_scatter(own_part, "tp", scatter_dimension=1, tiled=True)
        ).astype(jnp.bfloat16)
        ya_full = lax.all_gather(ya_sh, "tp", axis=1, tiled=True)
        spare_part = (
            successor_layer(ya_full)
            if tick_index == TICKS - 1
            else lax.cond(is_pred, lambda: successor_layer(ya_full), lambda: blank)
        )
        spare_sh = (
            ya_sh.astype(jnp.float32)
            + lax.psum_scatter(spare_part, "tp", scatter_dimension=1, tiled=True)
        ).astype(jnp.bfloat16)
        result_sh = jnp.where(is_pred, spare_sh, ya_sh)
        entering = lax.dynamic_index_in_dim(
            admissible_microbatches, arrival_plan[tick_index], 0, keepdims=False
        )
        send_sh = jnp.where(my_section == sections - 1, entering, result_sh)
        near_rows = shifted(send_sh, "section", 1)
        far_rows = shifted(spare_sh, "section", 2)
        x_sh = jnp.where(is_lost, jnp.zeros_like(far_rows), jnp.where(is_next, far_rows, near_rows))
        entire_source_lines = lax.all_gather(x_sh, "tp", axis=1, tiled=True)
        standby_sh = far_rows
    return (entire_source_lines[None], standby_sh[None])


def solution(mesh):
    placed = (
        P("section", None, None),
        P(None, None, "tp"),
        P(),
        P(),
        P("section", None, None, "tp"),
        P("section", "tp", None),
        P("section", None),
    )
    return jax.shard_map(
        per_device,
        mesh=mesh,
        in_specs=placed,
        out_specs=(P("section", None, None), P("section", None, "tp")),
        check_vma=False,
    )
```

profile of v0, /device:TPU:0, one launch (start us, length us, event | category | flops | bytes accessed | tf_op | source)
XLA Modules:
  0.0 769.3 jit_solution(308551706380850222)
XLA Ops:
  7.2 8.8 %copy.42 = bf16[1,4096,3,256]{1,3,2,0:T(8,128)(2,1)} copy(bf16[1,4096,3,256]{3,1,2,0:T(8,128)(2,1)} %param.15) | data formatting | bytes 12582912 | tf_op args[4]
  16.1 2.4 collective-permute-start.1
  18.5 0.6 iota_compare_fusion.2
  19.9 5.2 convolution_convert_fusion.7
  25.2 0.9 fusion.65
  26.5 1.8 fusion.103
  28.4 0.7 collective-permute-start.2
  29.1 68.7 %reduce-scatter.7.cloned.1.call-done = f32[128,512]{1,0:T(8,128)} async-done(((f32[128,4096]{1,0:T(8,128)}), f32[128,512]{1,0:T(8,128)}) %reduce-scatter.7.cloned.1.call-update) | async-done | bytes 262160 | tf_op jit(solution)/shard_map/reduce_scatter | solution.py:85
  97.8 1.6 fusion.86
  100.3 9.4 %collective-permute-done = bf16[4096]{0:T(1024)(128)(2,1)S(1)} collective-permute-done((bf16[4096]{0:T(1024)(128)(2,1)S(1)}, bf16[4096]{0:T(1024)(128)(2,1)S(1)}, u32[]{:S(2)}, u32[]{:S(2)}) %collective-permute-start) | collective-permute-done | bytes 8224 | tf_op jit(solution)/shard_map/ppermute | solution.py:14
  109.7 29.2 %all-gather.7.cloned.1.call-done = bf16[128,4096]{1,0:T(8,128)(2,1)} async-done(((bf16[128,512]{1,0:T(8,128)(2,1)}), bf16[128,4096]{1,0:T(8,128)(2,1)}) %all-gather.7.cloned.1.call-update) | async-done | bytes 1048592 | tf_op jit(solution)/shard_map/all_gather | solution.py:87
  138.9 12.4 %conditional.2 = (f32[128,4096]{1,0:T(8,128)}) conditional(s32[]{:T(128)} %convert_element_type.183, () %tuple.20, (bf16[128,4096]{1,0:T(8,128)(2,1)}, bf16[4096]{0:T(1024)(128)(2,1)S(1)}, bf16[4096,3,256]{0,2,1:T(8,128)(2,1)}, bf16[256,4096]{1,0:T(8,128)(2,1)}) %tuple.21), branch_computations={%region_5.6_spmd, %region_6.11_spmd} | conditional | flops 1096667776 | bytes 19741220 | solution.py:91
  138.9 1.5 convert_reduce_fusion
  140.5 1.7 fusion.3
  142.2 5.0 convolution_convert_fusion
  148.0 3.4 fusion.118
  151.5 0.6 copy-done.17
  152.0 0.7 fusion.113
  154.6 64.0 %reduce-scatter.9.cloned.1.call-done = f32[128,512]{1,0:T(8,128)} async-done(((f32[128,4096]{1,0:T(8,128)}), f32[128,512]{1,0:T(8,128)}) %reduce-scatter.9.cloned.1.call-update) | async-done | bytes 262160 | tf_op jit(solution)/shard_map/reduce_scatter | solution.py:95
  218.5 1.1 bitcast_select_fusion.2
  219.6 1.5 collective-permute-start.3
  221.2 4.0 collective-permute-done.3
  225.2 0.9 collective-permute-done.4
  226.1 0.7 select_select_fusion.2
  226.8 38.5 %all-gather.9.cloned.1.call-done = bf16[128,4096]{1,0:T(8,128)(2,1)} async-done(((bf16[128,512]{1,0:T(8,128)(2,1)}), bf16[128,4096]{1,0:T(8,128)(2,1)}) %all-gather.9.cloned.1.call-update) | async-done | bytes 1048592 | tf_op jit(solution)/shard_map/all_gather | solution.py:105
  265.3 1.5 convert_reduce_fusion.5
  266.9 1.7 fusion.48
  268.6 5.0 convolution_convert_fusion.6
  274.4 1.8 fusion.101
  276.2 68.0 %reduce-scatter.11.cloned.1.call-done = f32[128,512]{1,0:T(8,128)} async-done(((f32[128,4096]{1,0:T(8,128)}), f32[128,512]{1,0:T(8,128)}) %reduce-scatter.11.cloned.1.call-update) | async-done | bytes 262160 | tf_op jit(solution)/shard_map/reduce_scatter | solution.py:85
  344.2 1.6 add_convert_fusion.3
  346.0 39.2 %all-gather.11.cloned.1.call-done = bf16[128,4096]{1,0:T(8,128)(2,1)} async-done(((bf16[128,512]{1,0:T(8,128)(2,1)}), bf16[128,4096]{1,0:T(8,128)(2,1)}) %all-gather.11.cloned.1.call-update) | async-done | bytes 1048592 | tf_op jit(solution)/shard_map/all_gather | solution.py:87
  385.2 12.4 %conditional.3 = (f32[128,4096]{1,0:T(8,128)}) conditional(s32[]{:T(128)} %convert_element_type.183, () %tuple.22, (bf16[128,4096]{1,0:T(8,128)(2,1)}, bf16[4096]{0:T(1024)(128)(2,1)S(1)}, bf16[4096,3,256]{0,2,1:T(8,128)(2,1)}, bf16[256,4096]{1,0:T(8,128)(2,1)}) %tuple.23), branch_computations={%region_17.18_spmd, %region_18.23_spmd} | conditional | flops 1096667776 | bytes 19741220 | solution.py:91
  385.2 1.5 convert_reduce_fusion.1
  386.7 1.7 fusion.19
  388.4 5.0 convolution_convert_fusion.2
  394.2 3.4 fusion.119
  399.6 65.4 %reduce-scatter.13.cloned.1.call-done = f32[128,512]{1,0:T(8,128)} async-done(((f32[128,4096]{1,0:T(8,128)}), f32[128,512]{1,0:T(8,128)}) %reduce-scatter.13.cloned.1.call-update) | async-done | bytes 262160 | tf_op jit(solution)/shard_map/reduce_scatter | solution.py:95
  465.1 1.0 bitcast_select_fusion.1
  466.1 1.5 collective-permute-start.5
  467.6 4.0 collective-permute-done.5
  471.6 0.9 collective-permute-done.6
  472.5 0.7 select_select_fusion.1
  473.3 38.5 %all-gather.13.cloned.1.call-done = bf16[128,4096]{1,0:T(8,128)(2,1)} async-done(((bf16[128,512]{1,0:T(8,128)(2,1)}), bf16[128,4096]{1,0:T(8,128)(2,1)}) %all-gather.13.cloned.1.call-update) | async-done | bytes 1048592 | tf_op jit(solution)/shard_map/all_gather | solution.py:105
  511.8 1.5 convert_reduce_fusion.4
  513.3 1.7 fusion.45
  515.0 5.0 convolution_convert_fusion.5
  520.8 1.8 fusion.99
  522.7 68.3 %reduce-scatter.15.cloned.1.call-done = f32[128,512]{1,0:T(8,128)} async-done(((f32[128,4096]{1,0:T(8,128)}), f32[128,512]{1,0:T(8,128)}) %reduce-scatter.15.cloned.1.call-update) | async-done | bytes 262160 | tf_op jit(solution)/shard_map/reduce_scatter | solution.py:85
  591.0 1.6 add_convert_fusion.1
  592.7 39.2 %all-gather.15.cloned.1.call-done = bf16[128,4096]{1,0:T(8,128)(2,1)} async-done(((bf16[128,512]{1,0:T(8,128)(2,1)}), bf16[128,4096]{1,0:T(8,128)(2,1)}) %all-gather.15.cloned.1.call-update) | async-done | bytes 1048592 | tf_op jit(solution)/shard_map/all_gather | solution.py:87
  631.9 1.5 convert_reduce_fusion.3
  633.5 1.7 fusion.42
  635.2 5.0 convolution_convert_fusion.4
  640.9 3.4 fusion.120
  646.5 66.3 %reduce-scatter.17.cloned.1.call-done = f32[128,512]{1,0:T(8,128)} async-done(((f32[128,4096]{1,0:T(8,128)}), f32[128,512]{1,0:T(8,128)}) %reduce-scatter.17.cloned.1.call-update) | async-done | bytes 262160 | tf_op jit(solution)/shard_map/reduce_scatter | solution.py:95
  712.8 1.0 bitcast_select_fusion
  713.8 1.5 collective-permute-start.7
  715.3 4.1 collective-permute-done.7
  719.4 0.9 collective-permute-done.8
  720.2 0.7 select_select_fusion
  720.9 38.5 %all-gather.17.cloned.1.call-done = bf16[128,4096]{1,0:T(8,128)(2,1)} async-done(((bf16[128,512]{1,0:T(8,128)(2,1)}), bf16[128,4096]{1,0:T(8,128)(2,1)}) %all-gather.17.cloned.1.call-update) | async-done | bytes 1048592 | tf_op jit(solution)/shard_map/all_gather | solution.py:105
  759.5 2.3 copy.115
  761.8 0.7 copy.116
  (121 shorter events, 5.9 us)
Async XLA Ops:
  7.2 11.9 %copy-start.15 = (bf16[1,4096]{1,0:T(2,128)(2,1)S(1)}, bf16[1,4096]{1,0:T(2,128)(2,1)}, u32[]{:S(2)}) copy-start(bf16[1,4096]{1,0:T(2,128)(2,1)} %param.17) | copy-start | bytes 24580
  7.2 12.0 %copy-start.1 = (bf16[1,128,4096]{2,1,0:T(8,128)(2,1)S(1)}, bf16[1,128,4096]{2,1,0:T(8,128)(2,1)}, u32[]{:S(2)}) copy-start(bf16[1,128,4096]{2,1,0:T(8,128)(2,1)} %param.11) | copy-start | bytes 3145732
  7.2 90.7 %reduce-scatter.7.cloned.1.call-start = ((), (), s32[]{:S(2)}) async-start(), calls=%async_computation.6 | async-start | bytes 2359296 | tf_op jit(solution)/shard_map/reduce_scatter | solution.py:85
  16.1 122.9 %collective-permute-start.1 = (bf16[4096,3,256]{0,2,1:T(8,128)(2,1)}, bf16[4096,3,256]{0,2,1:T(8,128)(2,1)}, u32[]{:S(2)}, u32[]{:S(2)}) collective-permute-start(bf16[4096,3,256]{0,2,1:T(8,128)(2,1)} %bitcast.141), channel_id=1, source_target_pairs={{0,24},{8,0},{16,8},{24,16},{1,25},{9,1},{17,9},{25,17},{2,26},{10... | collective-permute-start | bytes 18874376 | tf_op jit(solution)/shard_map/ppermute | solution.py:14
  19.2 0.7 copy-start.13
  19.8 6.7 copy-start
  28.3 110.6 %all-gather.7.cloned.1.call-start = ((), (), s32[]{:S(2)}) async-start(), calls=%async_computation.7 | async-start | bytes 1179648 | tf_op jit(solution)/shard_map/all_gather | solution.py:87
  28.4 81.3 %collective-permute-start.2 = (bf16[256,4096]{1,0:T(8,128)(2,1)S(1)}, bf16[256,4096]{1,0:T(8,128)(2,1)}, u32[]{:S(2)}, u32[]{:S(2)}) collective-permute-start(bf16[256,4096]{1,0:T(8,128)(2,1)S(1)} %bitcast.140), channel_id=1, source_target_pairs={{0,24},{8,0},{16,8},{24,16},{1,25},{9,1},{17,9},{25,17},{2,26},{10... | collective-permute-start | bytes 6291464 | tf_op jit(solution)/shard_map/ppermute | solution.py:14
  99.5 119.0 %reduce-scatter.9.cloned.1.call-start = ((), (), s32[]{:S(2)}) async-start(), calls=%async_computation.8 | async-start | bytes 2359296 | tf_op jit(solution)/shard_map/reduce_scatter | solution.py:95
  99.6 10.2 %collective-permute-start = (bf16[4096]{0:T(1024)(128)(2,1)S(1)}, bf16[4096]{0:T(1024)(128)(2,1)S(1)}, u32[]{:S(2)}, u32[]{:S(2)}) collective-permute-start(bf16[4096]{0:T(1024)(128)(2,1)S(1)} %reduce.1), channel_id=1, source_target_pairs={{0,24},{8,0},{16,8},{24,16},{1,25},{9,1},{17,9},{25,17},{2,26},{10... | collective-permute-start | bytes 24584 | tf_op jit(solution)/shard_map/ppermute | solution.py:14
  138.9 3.2 copy-start.2
  151.4 0.7 copy-start.17
  151.4 67.2 %copy-start.7 = (bf16[128,512]{1,0:T(8,128)(2,1)S(1)}, bf16[128,512]{1,0:T(8,128)(2,1)}, u32[]{:S(2)}) copy-start(bf16[128,512]{1,0:T(8,128)(2,1)} %fusion.86) | copy-start | bytes 393220
  151.4 117.1 %copy-start.14 = (f32[4096]{0:T(1024)S(1)}, f32[4096]{0:T(1024)}, u32[]{:S(2)}) copy-start(f32[4096]{0:T(1024)} %copy-done.13) | copy-start | bytes 49156
  151.4 113.9 %all-gather.9.cloned.1.call-start = ((), (), s32[]{:S(2)}) async-start(), calls=%async_computation.9 | async-start | bytes 1179648 | tf_op jit(solution)/shard_map/all_gather | solution.py:105
  219.6 5.5 collective-permute-start.3
  221.2 4.9 collective-permute-start.4
  226.8 117.5 %reduce-scatter.11.cloned.1.call-start = ((), (), s32[]{:S(2)}) async-start(), calls=%async_computation.10 | async-start | bytes 2359296 | tf_op jit(solution)/shard_map/reduce_scatter | solution.py:85
  265.3 3.2 copy-start.6
  268.6 5.3 copy-start.16
  276.2 68.1 %copy-start.9 = (bf16[128,512]{1,0:T(8,128)(2,1)S(1)}, bf16[128,512]{1,0:T(8,128)(2,1)}, u32[]{:S(2)}) copy-start(bf16[128,512]{1,0:T(8,128)(2,1)} %select_select_fusion.2) | copy-start | bytes 393220
  276.2 109.0 %all-gather.11.cloned.1.call-start = ((), (), s32[]{:S(2)}) async-start(), calls=%async_computation.11 | async-start | bytes 1179648 | tf_op jit(solution)/shard_map/all_gather | solution.py:87
  345.9 119.2 %reduce-scatter.13.cloned.1.call-start = ((), (), s32[]{:S(2)}) async-start(), calls=%async_computation.12 | async-start | bytes 2359296 | tf_op jit(solution)/shard_map/reduce_scatter | solution.py:95
  385.2 3.2 copy-start.3
  397.6 67.5 %copy-start.10 = (bf16[128,512]{1,0:T(8,128)(2,1)S(1)}, bf16[128,512]{1,0:T(8,128)(2,1)}, u32[]{:S(2)}) copy-start(bf16[128,512]{1,0:T(8,128)(2,1)} %add_convert_fusion.3) | copy-start | bytes 393220
  397.6 67.5 %copy-start.12 = (bf16[4,128,512]{2,1,0:T(8,128)(2,1)S(1)}, bf16[4,128,512]{2,1,0:T(8,128)(2,1)}, u32[]{:S(2)}) copy-start(bf16[4,128,512]{2,1,0:T(8,128)(2,1)} %param.12) | copy-start | bytes 1572868
  397.6 114.2 %all-gather.13.cloned.1.call-start = ((), (), s32[]{:S(2)}) async-start(), calls=%async_computation.13 | async-start | bytes 1179648 | tf_op jit(solution)/shard_map/all_gather | solution.py:105
  466.1 5.5 collective-permute-start.5
  467.6 4.9 collective-permute-start.6
  473.2 117.7 %reduce-scatter.15.cloned.1.call-start = ((), (), s32[]{:S(2)}) async-start(), calls=%async_computation.14 | async-start | bytes 2359296 | tf_op jit(solution)/shard_map/reduce_scatter | solution.py:85
  511.8 3.2 copy-start.5
  522.6 68.4 %copy-start.8 = (bf16[128,512]{1,0:T(8,128)(2,1)S(1)}, bf16[128,512]{1,0:T(8,128)(2,1)}, u32[]{:S(2)}) copy-start(bf16[128,512]{1,0:T(8,128)(2,1)} %select_select_fusion.1) | copy-start | bytes 393220
  522.6 109.3 %all-gather.15.cloned.1.call-start = ((), (), s32[]{:S(2)}) async-start(), calls=%async_computation.15 | async-start | bytes 1179648 | tf_op jit(solution)/shard_map/all_gather | solution.py:87
  592.6 120.1 %reduce-scatter.17.cloned.1.call-start = ((), (), s32[]{:S(2)}) async-start(), calls=%async_computation.16 | async-start | bytes 2359296 | tf_op jit(solution)/shard_map/reduce_scatter | solution.py:95
  631.9 3.2 copy-start.4
  644.4 68.4 %copy-start.11 = (bf16[128,512]{1,0:T(8,128)(2,1)S(1)}, bf16[128,512]{1,0:T(8,128)(2,1)}, u32[]{:S(2)}) copy-start(bf16[128,512]{1,0:T(8,128)(2,1)} %add_convert_fusion.1) | copy-start | bytes 393220
  644.4 115.1 %all-gather.17.cloned.1.call-start = ((), (), s32[]{:S(2)}) async-start(), calls=%async_computation.17 | async-start | bytes 1179648 | tf_op jit(solution)/shard_map/all_gather | solution.py:105
  713.8 5.6 collective-permute-start.7
  715.3 4.9 collective-permute-start.8
Sparse Core Ops, SparseCore 0:
  28.5 69.3 reduce-scatter.6
  100.5 38.4 all-gather.6
  151.5 66.9 reduce-scatter.8
  226.9 38.3 all-gather.8
  276.3 67.8 reduce-scatter.10
  346.7 38.3 all-gather.10
  397.7 67.2 reduce-scatter.12
  473.4 38.3 all-gather.12
  522.8 68.1 reduce-scatter.14
  593.4 38.4 all-gather.14
  644.5 68.2 reduce-scatter.16
  721.0 38.3 all-gather.16
where the time goes:
time: 771 us; the launch traced here: 769 us
  waiting for transfers between devices  648 us (84%)
  matrix products  48.7 us (6%)
  other arithmetic  27.9 us (4%)
  between operations  21.1 us (3%)
  local copies, waits for them, and re-layouts  14.9 us (2%)
  starting transfers between devices  8.26 us (1%)
    reduce_scatter x3, waiting for transfers between devices, per_device(): lax.psum_scatter(own_part, 'tp', scatter_dimension=1, tiled=True)  205 us
    reduce_scatter x3, waiting for transfers between devices, per_device(): lax.psum_scatter(spare_part, 'tp', scatter_dimension=1, tiled=True)  196 us
    all_gather x3, waiting for transfers between devices, per_device(): entire_source_lines = lax.all_gather(x_sh, 'tp', axis=1, tiled=True)  116 us
    all_gather x3, waiting for transfers between devices, per_device(): ya_full = lax.all_gather(ya_sh, 'tp', axis=1, tiled=True)  108 us
    dot_general x6, matrix products, attend(): jnp.dot(normed, w_in.reshape(w_in.shape[0], 3 * col_count), preferred_ele...  30.3 us
    ppermute x9, waiting for transfers between devices, shifted(): return lax.ppermute(value, axis, pairs)  24.2 us
    dot_general x6, matrix products, attend(): return jnp.dot(context, w_out, preferred_element_type=jnp.float32)  15.6 us
  transfers between devices with their start and end apart: 21, of which 19 were waited for; matrix products, arithmetic and copies ran while one was open for 2% of the time, Pallas kernels for 0%

commit v1 on v0

--- a/solution.py
+++ b/solution.py
@@ -84,7 +84,9 @@
             x_sh.astype(jnp.float32)
             + lax.psum_scatter(own_part, "tp", scatter_dimension=1, tiled=True)
         ).astype(jnp.bfloat16)
-        ya_full = lax.all_gather(ya_sh, "tp", axis=1, tiled=True)
+        ya_full = jnp.concatenate(
+            lax.all_to_all(jnp.stack([ya_sh] * lax.axis_size("tp")), "tp", 0, 0), axis=1
+        )
         spare_part = (
             successor_layer(ya_full)
             if tick_index == TICKS - 1

time: 771 us -> 738 us (0.957)
  waiting for transfers between devices: 648 us -> 603 us
  starting transfers between devices: 8.26 us -> 19.7 us
    all_gather x3 -> x0, waiting for transfers between devices: 108 us -> none  [per_device(): ya_full = lax.all_gather(ya_sh, 'tp', axis=1, tiled=True)]
    all_to_all x0 -> x3, waiting for transfers between devices: none -> 67.6 us  [per_device(): lax.all_to_all(jnp.stack([ya_sh] * lax.axis_size('tp')), 'tp', 0, 0)]
    all_to_all x0 -> x3, starting transfers between devices: none -> 11 us  [per_device(): lax.all_to_all(jnp.stack([ya_sh] * lax.axis_size('tp')), 'tp', 0, 0)]
where the time goes in v1:
time: 738 us; the launch traced here: 736 us
  waiting for transfers between devices  603 us (82%)
  matrix products  48.7 us (7%)
  other arithmetic  25.3 us (3%)
  between operations  20.5 us (3%)
  starting transfers between devices  19.7 us (3%)
  local copies, waits for them, and re-layouts  19.1 us (3%)
    reduce_scatter x3, waiting for transfers between devices, per_device(): lax.psum_scatter(own_part, 'tp', scatter_dimension=1, tiled=True)  205 us
    reduce_scatter x3, waiting for transfers between devices, per_device(): lax.psum_scatter(spare_part, 'tp', scatter_dimension=1, tiled=True)  195 us
    all_gather x3, waiting for transfers between devices, per_device(): entire_source_lines = lax.all_gather(x_sh, 'tp', axis=1, tiled=True)  115 us
    all_to_all x3, waiting for transfers between devices, per_device(): lax.all_to_all(jnp.stack([ya_sh] * lax.axis_size('tp')), 'tp', 0, 0)  67.6 us
    dot_general x6, matrix products, attend(): jnp.dot(normed, w_in.reshape(w_in.shape[0], 3 * col_count), preferred_ele...  30.2 us
    ppermute x9, waiting for transfers between devices, shifted(): return lax.ppermute(value, axis, pairs)  19.7 us
    dot_general x6, matrix products, attend(): return jnp.dot(context, w_out, preferred_element_type=jnp.float32)  15.6 us
  transfers between devices with their start and end apart: 21, of which 19 were waited for; matrix products, arithmetic and copies ran while one was open for 2% of the time, Pallas kernels for 0%

profile of v1, /device:TPU:0, one launch (start us, length us, event | category | flops | bytes accessed | tf_op | source)
XLA Modules:
  0.0 736.5 jit_solution(14723783247843376894)
XLA Ops:
  7.2 8.8 %copy.69 = bf16[1,4096,3,256]{1,3,2,0:T(8,128)(2,1)} copy(bf16[1,4096,3,256]{3,1,2,0:T(8,128)(2,1)} %param.15) | data formatting | bytes 12582912 | tf_op args[4]
  16.1 2.4 collective-permute-start.1
  19.8 5.2 convolution_convert_fusion.7
  25.2 0.9 fusion.57
  26.5 1.8 fusion.91
  28.3 0.7 collective-permute-start.2
  29.1 69.1 %reduce-scatter.7.cloned.1.call-done = f32[128,512]{1,0:T(8,128)} async-done(((f32[128,4096]{1,0:T(8,128)}), f32[128,512]{1,0:T(8,128)}) %reduce-scatter.7.cloned.1.call-update) | async-done | bytes 262160 | tf_op jit(solution)/shard_map/reduce_scatter | solution.py:85
  98.1 1.0 fusion.74
  99.1 1.1 stack.6
  100.2 3.7 all-to-all-start
  104.6 5.1 collective-permute-done
  109.7 18.6 %all-to-all-done = bf16[8,128,512]{2,1,0:T(8,128)(2,1)S(1)} async-done(((bf16[8,128,512]{2,1,0:T(8,128)(2,1)}), bf16[8,128,512]{2,1,0:T(8,128)(2,1)S(1)}, u32[]{:S(2)}, u32[]{:S(2)}) %all-to-all-start) | async-done | bytes 1048608 | tf_op jit(solution)/shard_map/all_to_all | solution.py:88
  128.3 13.2 %conditional.2 = (f32[128,4096]{1,0:T(8,128)}) conditional(s32[]{:T(128)} %convert_element_type.194, () %tuple.20, (bf16[128,8,512]{2,0,1:T(8,128)(2,1)S(1)}, bf16[4096]{0:T(1024)(128)(2,1)S(1)}, bf16[4096,3,256]{0,2,1:T(8,128)(2,1)}, bf16[256,4096]{1,0:T(8,128)(2,1)}) %tuple.68), branch_computations={%region_5.6_spmd, %region_6.11_spmd} | conditional | flops 1096663680 | bytes 19741192 | solution.py:93
  128.3 1.0 convert_reduce_fusion
  129.4 1.9 fusion.3
  132.4 5.0 convolution_convert_fusion
  138.2 3.4 fusion.106
  144.8 63.7 %reduce-scatter.9.cloned.1.call-done = f32[128,512]{1,0:T(8,128)} async-done(((f32[128,4096]{1,0:T(8,128)}), f32[128,512]{1,0:T(8,128)}) %reduce-scatter.9.cloned.1.call-update) | async-done | bytes 262160 | tf_op jit(solution)/shard_map/reduce_scatter | solution.py:97
  208.5 1.1 bitcast_select_fusion.2
  209.6 1.5 collective-permute-start.3
  211.1 4.0 collective-permute-done.3
  215.1 0.9 collective-permute-done.4
  216.0 0.7 select_select_fusion.2
  217.0 38.4 %all-gather.4.cloned.1.call-done = bf16[128,4096]{1,0:T(8,128)(2,1)} async-done(((bf16[128,512]{1,0:T(8,128)(2,1)}), bf16[128,4096]{1,0:T(8,128)(2,1)}) %all-gather.4.cloned.1.call-update) | async-done | bytes 1048592 | tf_op jit(solution)/shard_map/all_gather | solution.py:107
  255.3 1.5 convert_reduce_fusion.5
  256.9 1.7 fusion.40
  258.6 5.0 convolution_convert_fusion.6
  264.4 1.8 fusion.89
  266.2 68.0 %reduce-scatter.11.cloned.1.call-done = f32[128,512]{1,0:T(8,128)} async-done(((f32[128,4096]{1,0:T(8,128)}), f32[128,512]{1,0:T(8,128)}) %reduce-scatter.11.cloned.1.call-update) | async-done | bytes 262160 | tf_op jit(solution)/shard_map/reduce_scatter | solution.py:85
  334.2 1.0 add_convert_fusion.3
  335.2 1.1 stack.7
  336.2 3.7 all-to-all-start.1
  339.9 24.5 %all-to-all-done.1 = bf16[8,128,512]{2,1,0:T(8,128)(2,1)S(1)} async-done(((bf16[8,128,512]{2,1,0:T(8,128)(2,1)}), bf16[8,128,512]{2,1,0:T(8,128)(2,1)S(1)}, u32[]{:S(2)}, u32[]{:S(2)}) %all-to-all-start.1) | async-done | bytes 1048608 | tf_op jit(solution)/shard_map/all_to_all | solution.py:88
  364.5 13.2 %conditional.3 = (f32[128,4096]{1,0:T(8,128)}) conditional(s32[]{:T(128)} %convert_element_type.194, () %tuple.22, (bf16[128,8,512]{2,0,1:T(8,128)(2,1)S(1)}, bf16[4096]{0:T(1024)(128)(2,1)S(1)}, bf16[4096,3,256]{0,2,1:T(8,128)(2,1)}, bf16[256,4096]{1,0:T(8,128)(2,1)}) %tuple.69), branch_computations={%region_17.18_spmd, %region_18.23_spmd} | conditional | flops 1096663680 | bytes 19741192 | solution.py:93
  364.5 1.0 convert_reduce_fusion.1
  365.5 1.9 fusion.15
  368.5 5.0 convolution_convert_fusion.2
  374.3 3.4 fusion.107
  379.5 65.2 %reduce-scatter.13.cloned.1.call-done = f32[128,512]{1,0:T(8,128)} async-done(((f32[128,4096]{1,0:T(8,128)}), f32[128,512]{1,0:T(8,128)}) %reduce-scatter.13.cloned.1.call-update) | async-done | bytes 262160 | tf_op jit(solution)/shard_map/reduce_scatter | solution.py:97
  444.7 1.0 bitcast_select_fusion.1
  445.7 1.5 collective-permute-start.5
  447.2 4.0 collective-permute-done.5
  451.2 0.9 collective-permute-done.6
  452.1 0.7 select_select_fusion.1
  453.1 38.3 %all-gather.6.cloned.1.call-done = bf16[128,4096]{1,0:T(8,128)(2,1)} async-done(((bf16[128,512]{1,0:T(8,128)(2,1)}), bf16[128,4096]{1,0:T(8,128)(2,1)}) %all-gather.6.cloned.1.call-update) | async-done | bytes 1048592 | tf_op jit(solution)/shard_map/all_gather | solution.py:107
  491.4 1.5 convert_reduce_fusion.4
  493.0 1.7 fusion.37
  494.6 5.0 convolution_convert_fusion.5
  500.4 1.8 fusion.87
  502.3 68.4 %reduce-scatter.15.cloned.1.call-done = f32[128,512]{1,0:T(8,128)} async-done(((f32[128,4096]{1,0:T(8,128)}), f32[128,512]{1,0:T(8,128)}) %reduce-scatter.15.cloned.1.call-update) | async-done | bytes 262160 | tf_op jit(solution)/shard_map/reduce_scatter | solution.py:85
  570.6 1.0 add_convert_fusion.1
  571.7 1.1 stack.8
  572.9 3.6 all-to-all-start.2
  576.6 24.5 %all-to-all-done.2 = bf16[8,128,512]{1,2,0:T(8,128)(2,1)S(1)} async-done(((bf16[8,128,512]{1,2,0:T(8,128)(2,1)}), bf16[8,128,512]{1,2,0:T(8,128)(2,1)S(1)}, u32[]{:S(2)}, u32[]{:S(2)}) %all-to-all-start.2) | async-done | bytes 1048608 | tf_op jit(solution)/shard_map/all_to_all | solution.py:88
  602.2 0.7 fusion.36
  602.9 5.0 convolution_convert_fusion.4
  608.7 3.4 fusion.108
  614.2 66.1 %reduce-scatter.17.cloned.1.call-done = f32[128,512]{1,0:T(8,128)} async-done(((f32[128,4096]{1,0:T(8,128)}), f32[128,512]{1,0:T(8,128)}) %reduce-scatter.17.cloned.1.call-update) | async-done | bytes 262160 | tf_op jit(solution)/shard_map/reduce_scatter | solution.py:97
  680.3 1.0 bitcast_select_fusion
  681.3 1.7 collective-permute-start.7
  683.0 3.7 collective-permute-done.7
  686.7 1.0 collective-permute-done.8
  688.4 38.6 %all-gather.8.cloned.1.call-done = bf16[128,4096]{1,0:T(8,128)(2,1)} async-done(((bf16[128,512]{1,0:T(8,128)(2,1)}), bf16[128,4096]{1,0:T(8,128)(2,1)}) %all-gather.8.cloned.1.call-update) | async-done | bytes 1048592 | tf_op jit(solution)/shard_map/all_gather | solution.py:107
  727.0 2.3 copy.153
  (115 shorter events, 12.6 us)
Async XLA Ops:
  7.2 11.9 %copy-start.9 = (bf16[1,4096]{1,0:T(2,128)(2,1)S(1)}, bf16[1,4096]{1,0:T(2,128)(2,1)}, u32[]{:S(2)}) copy-start(bf16[1,4096]{1,0:T(2,128)(2,1)} %param.17) | copy-start | bytes 24580
  7.2 12.0 %copy-start.1 = (bf16[1,128,4096]{2,1,0:T(8,128)(2,1)S(1)}, bf16[1,128,4096]{2,1,0:T(8,128)(2,1)}, u32[]{:S(2)}) copy-start(bf16[1,128,4096]{2,1,0:T(8,128)(2,1)} %param.11) | copy-start | bytes 3145732
  7.2 90.9 %reduce-scatter.7.cloned.1.call-start = ((), (), s32[]{:S(2)}) async-start(), calls=%async_computation.9 | async-start | bytes 2359296 | tf_op jit(solution)/shard_map/reduce_scatter | solution.py:85
  16.1 112.3 %collective-permute-start.1 = (bf16[4096,3,256]{0,2,1:T(8,128)(2,1)}, bf16[4096,3,256]{0,2,1:T(8,128)(2,1)}, u32[]{:S(2)}, u32[]{:S(2)}) collective-permute-start(bf16[4096,3,256]{0,2,1:T(8,128)(2,1)} %bitcast.155), channel_id=1, source_target_pairs={{0,24},{8,0},{16,8},{24,16},{1,25},{9,1},{17,9},{25,17},{2,26},{10... | collective-permute-start | bytes 18874376 | tf_op jit(solution)/shard_map/ppermute | solution.py:14
  19.1 0.7 copy-start.7
  19.8 6.7 copy-start
  28.3 81.4 %collective-permute-start.2 = (bf16[256,4096]{1,0:T(8,128)(2,1)S(1)}, bf16[256,4096]{1,0:T(8,128)(2,1)}, u32[]{:S(2)}, u32[]{:S(2)}) collective-permute-start(bf16[256,4096]{1,0:T(8,128)(2,1)S(1)} %bitcast.152), channel_id=1, source_target_pairs={{0,24},{8,0},{16,8},{24,16},{1,25},{9,1},{17,9},{25,17},{2,26},{10... | collective-permute-start | bytes 6291464 | tf_op jit(solution)/shard_map/ppermute | solution.py:14
  100.2 28.2 %all-to-all-start = ((bf16[8,128,512]{2,1,0:T(8,128)(2,1)}), bf16[8,128,512]{2,1,0:T(8,128)(2,1)S(1)}, u32[]{:S(2)}, u32[]{:S(2)}) async-start(bf16[8,128,512]{2,1,0:T(8,128)(2,1)} %stack.6), calls=%async_computation.1 | async-start | bytes 2097152 | tf_op jit(solution)/shard_map/all_to_all | solution.py:88
  103.8 104.7 %reduce-scatter.9.cloned.1.call-start = ((), (), s32[]{:S(2)}) async-start(), calls=%async_computation.10 | async-start | bytes 2359296 | tf_op jit(solution)/shard_map/reduce_scatter | solution.py:97
  103.9 5.9 collective-permute-start
  141.6 0.7 copy-start.11
  141.6 116.9 %copy-start.8 = (f32[4096]{0:T(1024)S(1)}, f32[4096]{0:T(1024)}, u32[]{:S(2)}) copy-start(f32[4096]{0:T(1024)} %copy-done.7) | copy-start | bytes 49156
  141.6 113.7 %all-gather.4.cloned.1.call-start = ((), (), s32[]{:S(2)}) async-start(), calls=%async_computation.11 | async-start | bytes 1179648 | tf_op jit(solution)/shard_map/all_gather | solution.py:107
  209.6 5.6 collective-permute-start.3
  211.1 4.9 collective-permute-start.4
  216.7 117.5 %reduce-scatter.11.cloned.1.call-start = ((), (), s32[]{:S(2)}) async-start(), calls=%async_computation.12 | async-start | bytes 2359296 | tf_op jit(solution)/shard_map/reduce_scatter | solution.py:85
  255.3 3.2 copy-start.3
  258.5 5.2 copy-start.10
  266.2 68.0 %copy-start.5 = (bf16[128,512]{1,0:T(8,128)(2,1)S(1)}, bf16[128,512]{1,0:T(8,128)(2,1)}, u32[]{:S(2)}) copy-start(bf16[128,512]{1,0:T(8,128)(2,1)} %select_select_fusion.2) | copy-start | bytes 393220
  336.2 28.2 %all-to-all-start.1 = ((bf16[8,128,512]{2,1,0:T(8,128)(2,1)}), bf16[8,128,512]{2,1,0:T(8,128)(2,1)S(1)}, u32[]{:S(2)}, u32[]{:S(2)}) async-start(bf16[8,128,512]{2,1,0:T(8,128)(2,1)} %stack.7), calls=%async_computation.4 | async-start | bytes 2097152 | tf_op jit(solution)/shard_map/all_to_all | solution.py:88
  339.9 104.8 %reduce-scatter.13.cloned.1.call-start = ((), (), s32[]{:S(2)}) async-start(), calls=%async_computation.13 | async-start | bytes 2359296 | tf_op jit(solution)/shard_map/reduce_scatter | solution.py:97
  377.7 67.0 %copy-start.6 = (bf16[4,128,512]{2,1,0:T(8,128)(2,1)S(1)}, bf16[4,128,512]{2,1,0:T(8,128)(2,1)}, u32[]{:S(2)}) copy-start(bf16[4,128,512]{2,1,0:T(8,128)(2,1)} %param.12) | copy-start | bytes 1572868
  377.7 113.7 %all-gather.6.cloned.1.call-start = ((), (), s32[]{:S(2)}) async-start(), calls=%async_computation.14 | async-start | bytes 1179648 | tf_op jit(solution)/shard_map/all_gather | solution.py:107
  445.7 5.5 collective-permute-start.5
  447.2 4.9 collective-permute-start.6
  452.8 117.8 %reduce-scatter.15.cloned.1.call-start = ((), (), s32[]{:S(2)}) async-start(), calls=%async_computation.15 | async-start | bytes 2359296 | tf_op jit(solution)/shard_map/reduce_scatter | solution.py:85
  491.4 3.2 copy-start.2
  502.3 68.4 %copy-start.4 = (bf16[128,512]{1,0:T(8,128)(2,1)S(1)}, bf16[128,512]{1,0:T(8,128)(2,1)}, u32[]{:S(2)}) copy-start(bf16[128,512]{1,0:T(8,128)(2,1)} %select_select_fusion.1) | copy-start | bytes 393220
  572.9 28.2 %all-to-all-start.2 = ((bf16[8,128,512]{1,2,0:T(8,128)(2,1)}), bf16[8,128,512]{1,2,0:T(8,128)(2,1)S(1)}, u32[]{:S(2)}, u32[]{:S(2)}) async-start(bf16[8,128,512]{1,2,0:T(8,128)(2,1)} %stack.8), calls=%async_computation.7 | async-start | bytes 2097152 | tf_op jit(solution)/shard_map/all_to_all | solution.py:88
  576.5 103.8 %reduce-scatter.17.cloned.1.call-start = ((), (), s32[]{:S(2)}) async-start(), calls=%async_computation.16 | async-start | bytes 2359296 | tf_op jit(solution)/shard_map/reduce_scatter | solution.py:97
  612.1 114.9 %all-gather.8.cloned.1.call-start = ((), (), s32[]{:S(2)}) async-start(), calls=%async_computation.17 | async-start | bytes 1179648 | tf_op jit(solution)/shard_map/all_gather | solution.py:107
  681.3 5.4 collective-permute-start.7
  683.0 4.7 collective-permute-start.8
Sparse Core Ops, SparseCore 0:
  28.5 69.6 reduce-scatter.6
  141.7 66.7 reduce-scatter.8
  216.8 38.4 all-gather.3
  266.3 67.8 reduce-scatter.10
  377.9 66.7 reduce-scatter.12
  453.0 38.4 all-gather.5
  502.4 68.1 reduce-scatter.14
  612.2 68.0 reduce-scatter.16
  688.6 38.4 all-gather.7
